TPU v7x, 32 devices: a whole 2x2x4 slice. The times are simulated.
32 devices in a mesh: gx: 16 (over z, y, x), gy: 2 (over core).
Axes of the slice: x: 2, y: 2, z: 4, core: 2. Of those that a mesh axis runs over, the one named last changes fastest.
Arguments:
- residual: bfloat16 [16, 2, 2048, 384], P('gx', 'gy'), may hold values from -6 to 6
- local_inverse: bfloat16 [16, 2, 2048, 2048], P('gx', 'gy'), may hold values from -0.125 to 0.125
- primal_basis: bfloat16 [16, 2, 96, 2048], P('gx', 'gy'), may hold values from -0.125 to 0.125
- row_stiffness: bfloat16 [16, 2, 2048], P('gx', 'gy'), may hold values from 0.099609375 to 10
- face_sizes: int32 [16, 2, 4], P('gx', 'gy'), may hold values from 0 to 512, as said below
- primal_slots: int32 [16, 2, 96], P('gx', 'gy'), may hold values from 0 to 287
- block_inverse: float32 [16, 2, 32, 64], P('gx', 'gy'), may hold values from -1 to 3
- level_basis: float32 [16, 2, 32, 64], P('gx', 'gy'), may hold values from -0.15625 to 0.15625
- top_inverse: float32 [64, 64], replicated, may hold values from -1 to 3
Outputs:
- preconditioned: bfloat16 [16, 2, 2048, 384], P('gx', 'gy')
Inputs may be any that keep to these rules, and one draw needn't show every extreme that they name: face_sizes[x, y, f] is equal on the two sides of a shared face, 0 on faces at the grid's edge, at least 128 elsewhere; the value 512 is reached.
All inputs are finite; a program needn't handle non-finite values.
Results may differ from a plain program's by a relative error of at most 0.008.
Values may be sent and summed in bfloat16 or wider, within the bound.
No kernel may reach another device: no remote copies, remote signals or barrier semaphores. Data moves between devices by JAX's collectives and lax.ppermute only.
A program may use at most 64 MiB of HBM per device.

v0:
```python
import jax
import jax.numpy as jnp
from jax import lax
from jax.sharding import PartitionSpec as P


def passed_along(block, axis, distance):
    devices = range(lax.axis_size(axis))
    route = [(i - distance, i) for i in devices if i - distance in devices]
    return lax.ppermute(block, axis, route)


def extended(block, sides, width):
    for axis, dim in sides:
        count = lax.axis_size(axis)
        forward = [(i, i + 1) for i in range(count - 1)]
        backward = [(target, source) for source, target in forward]
        low = lax.ppermute(
            lax.slice_in_dim(block, block.shape[dim] - width, None, axis=dim), axis, forward
        )
        high = lax.ppermute(lax.slice_in_dim(block, 0, width, axis=dim), axis, backward)
        block = jnp.concatenate([low, block, high], axis=dim)
    return block


def coarse_lift(phi_block, values, stiffness_block):
    coarse_rows = jnp.einsum("pw,pr->wr", phi_block, values, precision=lax.Precision.HIGHEST)
    return stiffness_block[:, None] * coarse_rows


def local(
    residual,
    local_inverse,
    primal_basis,
    row_stiffness,
    face_sizes,
    primal_slots,
    block_inverse,
    level_basis,
    top_inverse,
):
    highest = lax.Precision.HIGHEST
    own_rows = residual[0, 0]
    row_count = own_rows.shape[0]
    face_rows = row_count // 4
    coarse_count = block_inverse.shape[2]
    counts = face_sizes[0, 0]
    position = jnp.arange(row_count, dtype=jnp.int32)
    face_of_row = position // face_rows
    picked = jnp.where(
        face_of_row[:, None] == jnp.arange(4, dtype=jnp.int32)[None, :], counts[None, :], 0
    )
    live_rows = position % face_rows < jnp.sum(picked, axis=1)
    masked = jnp.where(live_rows[:, None], own_rows, jnp.zeros((), jnp.bfloat16))
    local_part = jnp.dot(local_inverse[0, 0], masked, preferred_element_type=jnp.float32)
    primal_phi = primal_basis[0, 0]
    partial_value = jnp.dot(primal_phi, masked, preferred_element_type=jnp.float32)
    selector = (
        primal_slots[0, 0][:, None] == jnp.arange(9 * coarse_count, dtype=jnp.int32)[None, :]
    ).astype(jnp.float32)
    spread = jnp.einsum("ps,pr->sr", selector, partial_value, precision=highest).reshape(
        3, 3, coarse_count, -1
    )
    from_below_y = passed_along(spread[:, 2], "gy", 1)
    from_above_y = passed_along(spread[:, 0], "gy", -1)
    along_x = spread[:, 1] + from_below_y + from_above_y
    from_below_x = passed_along(along_x[2], "gx", 1)
    from_above_x = passed_along(along_x[0], "gx", -1)
    assembled = along_x[1] + from_below_x + from_above_x
    level_phi = level_basis[0, 0]
    top_rhs = lax.psum(
        jnp.einsum("cl,cr->lr", level_phi, assembled, precision=highest), ("gx", "gy")
    )
    top_value = jnp.dot(top_inverse, top_rhs, precision=highest)
    block_rhs = lax.all_gather(assembled, "gy", axis=0, tiled=True)
    coarse = jnp.dot(block_inverse[0, 0], block_rhs, precision=highest) + jnp.dot(
        level_phi, top_value, precision=highest
    )
    beside_all = extended(coarse[None, None], (("gx", 0), ("gy", 1)), 1)
    primal_values = jnp.dot(selector, beside_all.reshape(9 * coarse_count, -1), precision=highest)
    stiffness = row_stiffness[0, 0]
    stiffness_f = stiffness.astype(jnp.float32)
    phi_f = primal_phi.astype(jnp.float32)
    local_weighted = jnp.where(live_rows[:, None], stiffness_f[:, None] * local_part, 0.0)
    own_total = local_weighted + coarse_lift(phi_f, primal_values, stiffness_f)
    sent = jnp.where(live_rows[:, None], own_total, 0.0).astype(jnp.bfloat16)

    def face_parts(values):
        return [values[face_id * face_rows : (face_id + 1) * face_rows] for face_id in range(4)]

    stiff_faces = face_parts(stiffness)
    sent_faces = face_parts(sent)
    recv_low_x = passed_along((sent_faces[1], stiff_faces[1]), "gx", 1)
    recv_high_x = passed_along((sent_faces[0], stiff_faces[0]), "gx", -1)
    recv_low_y = passed_along((sent_faces[3], stiff_faces[3]), "gy", 1)
    recv_high_y = passed_along((sent_faces[2], stiff_faces[2]), "gy", -1)
    received = [recv_low_x, recv_high_x, recv_low_y, recv_high_y]
    other_sent = jnp.concatenate([item[0] for item in received], axis=0)
    other_stiffness = jnp.concatenate([item[1] for item in received], axis=0)
    summed = sent.astype(jnp.float32) + other_sent.astype(jnp.float32)
    divisor = stiffness_f + other_stiffness.astype(jnp.float32)
    result = jnp.where(live_rows[:, None], summed / divisor[:, None], 0.0).astype(jnp.bfloat16)
    return result[None, None]


def solution(mesh):
    in_specs = (
        P("gx", "gy", None, None),
        P("gx", "gy", None, None),
        P("gx", "gy", None, None),
        P("gx", "gy", None),
        P("gx", "gy", None),
        P("gx", "gy", None),
        P("gx", "gy", None, None),
        P("gx", "gy", None, None),
        P(),
    )
    out_specs = P("gx", "gy", None, None)
    return jax.shard_map(local, mesh=mesh, in_specs=in_specs, out_specs=out_specs, check_vma=False)
```

profile of v0, /device:TPU:7, one launch (start us, length us, event | category | flops | bytes accessed | tf_op | source)
XLA Modules:
  0.0 229.3 jit_solution(7290555290257131025)
XLA Ops:
  7.6 2.4 %fusion.7 = f32[384,96]{1,0:T(8,128)S(1)} fusion(bf16[1,1,2048,384]{3,2,1,0:T(8,128)(2,1)} %param.9, pred[2048]{0:T(1024)(128)(4,1)S(1)} %fusion.29, bf16[1,1,96,2048]{3,2,1,0:T(8,128)(2,1)S(1)} %copy-done), kind=kOutput, calls=%fused_computation.5 | convolution fusion | flops 151781376 | bytes 2115584 | tf_op jit(solution)/shard_map/dot_general | solution.py:57
  10.5 1.3 collective-permute-start
  11.8 3.0 %collective-permute-start.1 = (f32[3,32,384]{2,1,0:T(8,128)S(1)}, f32[3,32,384]{2,1,0:T(8,128)S(1)}, u32[]{:S(2)}, u32[]{:S(2)}) collective-permute-start(f32[3,32,384]{2,1,0:T(8,128)S(1)} %get-tuple-element.14), channel_id=1, source_target_pairs={{1,0},{3,2},{5,4},{7,6},{9,8},{11,10},{13,12},{15,14},{17,16},{19,... | collective-permute-start | bytes 442376 | tf_op jit(solution)/shard_map/ppermute | solution.py:10
  14.8 1.0 collective-permute-done.1
  15.8 3.1 %collective-permute-start.2 = (f32[32,384]{1,0:T(8,128)S(1)}, f32[32,384]{1,0:T(8,128)S(1)}, u32[]{:S(2)}, u32[]{:S(2)}) collective-permute-start(f32[32,384]{1,0:T(8,128)S(1)} %get-tuple-element.15), channel_id=1, source_target_pairs={{0,2},{2,4},{4,6},{6,8},{8,10},{10,12},{12,14},{14,16},{16,18},{18... | collective-permute-start | bytes 147464 | tf_op jit(solution)/shard_map/ppermute | solution.py:10
  19.0 2.2 collective-permute-start.3
  21.1 4.5 %collective-permute-done.3 = f32[32,384]{1,0:T(8,128)S(1)} collective-permute-done((f32[32,384]{1,0:T(8,128)S(1)}, f32[32,384]{1,0:T(8,128)S(1)}, u32[]{:S(2)}, u32[]{:S(2)}) %collective-permute-start.3) | collective-permute-done | bytes 49184 | tf_op jit(solution)/shard_map/ppermute | solution.py:10
  25.6 1.2 convolution_bitcast_fusion
  26.8 3.3 %all_gather.3 = f32[64,384]{1,0:T(8,128)S(1)} all-gather(f32[32,384]{1,0:T(8,128)S(1)} %fusion.24), channel_id=1, replica_groups=mesh['gx'=16,'gy'=2] {'gy'}, dimensions={0}, use_global_device_ids=true | all-gather | bytes 147456 | tf_op jit(solution)/shard_map/all_gather | solution.py:75
  30.1 121.2 %all-reduce.2.cloned.1.call-done = f32[64,384]{0,1:T(8,128)} async-done(((f32[64,384]{0,1:T(8,128)}), f32[64,384]{0,1:T(8,128)}) %all-reduce.2.cloned.1.call-update) | async-done | bytes 98320 | tf_op jit(solution)/shard_map/psum | solution.py:71
  151.4 1.2 fusion.38
  153.2 4.6 %collective-permute-start.4 = (f32[1,1,32,384]{3,2,1,0:T(8,128)S(1)}, f32[1,1,32,384]{3,2,1,0:T(8,128)S(1)}, u32[]{:S(2)}, u32[]{:S(2)}) collective-permute-start(f32[1,1,32,384]{3,2,1,0:T(8,128)S(1)} %fusion.11), channel_id=1, source_target_pairs={{0,2},{2,4},{4,6},{6,8},{8,10},{10,12},{12,14},{14,16},{16,18},{18... | collective-permute-start | bytes 147464 | tf_op jit(solution)/shard_map/ppermute | solution.py:18
  157.8 1.9 collective-permute-start.5
  159.7 4.7 %collective-permute-done.5 = f32[1,1,32,384]{3,2,1,0:T(8,128)S(1)} collective-permute-done((f32[1,1,32,384]{3,2,1,0:T(8,128)S(1)}, f32[1,1,32,384]{3,2,1,0:T(8,128)S(1)}, u32[]{:S(2)}, u32[]{:S(2)}) %collective-permute-start.5) | collective-permute-done | bytes 49184 | tf_op jit(solution)/shard_map/ppermute | solution.py:21
  164.5 1.3 collective-permute-start.6
  165.8 5.9 %collective-permute-start.7 = (f32[3,1,32,384]{3,2,1,0:T(8,128)S(1)}, f32[3,1,32,384]{3,2,1,0:T(8,128)S(1)}, u32[]{:S(2)}, u32[]{:S(2)}) collective-permute-start(f32[3,1,32,384]{3,2,1,0:T(8,128)S(1)} %pad_maximum_fusion.1), channel_id=1, source_target_pairs={{1,0},{3,2},{5,4},{7,6},{9,8},{11,10},{13,12},{15,14},{17,16},{19,... | collective-permute-start | bytes 442376 | tf_op jit(solution)/shard_map/ppermute | solution.py:21
  171.7 0.9 collective-permute-done.7
  173.1 1.4 fusion.12
  174.6 7.5 %fusion.4 = bf16[2048,384]{0,1:T(8,128)(2,1)S(1)} fusion(f32[384,2048]{1,0:T(8,128)S(1)} %fusion.12, bf16[1,1,2048,2048]{3,2,1,0:T(8,128)(2,1)} %param.10, f32[2048]{0:T(1024)S(1)} %bitcast.75, pred[2048]{0:T(1024)(128)(4,1)S(1)} %fusion.29, bf16[1,1,2048,384]{3,2,1,0:T(8,128)(2,1)S(1)} %copy-done.6), kind=kOutput, calls=%fused_computation.4 | convolution fusion | flops 3226730496 | bytes 14690304 | tf_op jit(solution)/shard_map/dot_general | solution.py:55
  182.2 1.3 collective-permute-start.10
  183.5 3.1 %collective-permute-start.11 = (bf16[512,384]{0,1:T(8,128)(2,1)S(1)}, bf16[512,384]{0,1:T(8,128)(2,1)S(1)}, u32[]{:S(2)}, u32[]{:S(2)}) collective-permute-start(bf16[512,384]{0,1:T(8,128)(2,1)S(1)} %get-tuple-element.10), channel_id=1, source_target_pairs={{1,0},{3,2},{5,4},{7,6},{9,8},{11,10},{13,12},{15,14},{17,16},{19,... | collective-permute-start | bytes 1179656 | tf_op jit(solution)/shard_map/ppermute | solution.py:10
  186.6 1.9 collective-permute-start.8
  188.5 3.4 %collective-permute-start.9 = (bf16[512,384]{0,1:T(8,128)(2,1)S(1)}, bf16[512,384]{0,1:T(8,128)(2,1)S(1)}, u32[]{:S(2)}, u32[]{:S(2)}) collective-permute-start(bf16[512,384]{0,1:T(8,128)(2,1)S(1)} %get-tuple-element.12), channel_id=1, source_target_pairs={{2,0},{4,2},{6,4},{8,6},{10,8},{12,10},{14,12},{16,14},{18,16},{20... | collective-permute-start | bytes 1179656 | tf_op jit(solution)/shard_map/ppermute | solution.py:10
  191.9 3.7 %collective-permute-start.12 = (bf16[512]{0:T(512)(128)(2,1)S(1)}, bf16[512]{0:T(512)(128)(2,1)S(1)}, u32[]{:S(2)}, u32[]{:S(2)}) collective-permute-start(bf16[512]{0:T(512)(128)(2,1)S(1)} %get-tuple-element.5), channel_id=1, source_target_pairs={{0,2},{2,4},{4,6},{6,8},{8,10},{10,12},{12,14},{14,16},{16,18},{18... | collective-permute-start | bytes 3080 | tf_op jit(solution)/shard_map/ppermute | solution.py:10
  195.6 12.1 %collective-permute-done.12 = bf16[512]{0:T(512)(128)(2,1)S(1)} collective-permute-done((bf16[512]{0:T(512)(128)(2,1)S(1)}, bf16[512]{0:T(512)(128)(2,1)S(1)}, u32[]{:S(2)}, u32[]{:S(2)}) %collective-permute-start.12) | collective-permute-done | bytes 1056 | tf_op jit(solution)/shard_map/ppermute | solution.py:10
  207.7 1.9 collective-permute-start.13
  209.6 4.2 %collective-permute-done.13 = bf16[512]{0:T(512)(128)(2,1)S(1)} collective-permute-done((bf16[512]{0:T(512)(128)(2,1)S(1)}, bf16[512]{0:T(512)(128)(2,1)S(1)}, u32[]{:S(2)}, u32[]{:S(2)}) %collective-permute-start.13) | collective-permute-done | bytes 1056 | tf_op jit(solution)/shard_map/ppermute | solution.py:10
  213.8 1.3 collective-permute-start.14
  215.1 2.2 collective-permute-done.14
  217.3 2.1 collective-permute-start.15
  219.3 0.8 collective-permute-done.15
  220.8 1.6 copy.15
  (42 shorter events, 3.3 us)
Async XLA Ops:
  6.5 1.0 copy-start
  6.5 3.4 %copy-start.5 = (s32[1,1,96]{2,1,0:T(1,128)S(1)}, s32[1,1,96]{2,1,0:T(1,128)}, u32[]{:S(2)}) copy-start(s32[1,1,96]{2,1,0:T(1,128)} %param.14) | copy-start | bytes 1156
  6.5 19.1 %copy-start.1 = (f32[1,1,32,64]{3,2,1,0:T(8,128)S(1)}, f32[1,1,32,64]{3,2,1,0:T(8,128)}, u32[]{:S(2)}) copy-start(f32[1,1,32,64]{3,2,1,0:T(8,128)} %param.16) | copy-start | bytes 24580
  6.5 144.8 %all-reduce.2.cloned.1.call-start = ((), (), s32[]{:S(2)}) async-start(), calls=%async_computation | async-start | bytes 393216 | tf_op jit(solution)/shard_map/psum | solution.py:71
  7.5 143.8 %copy-start.3 = (f32[64,64]{1,0:T(8,128)S(1)}, f32[64,64]{1,0:T(8,128)}, u32[]{:S(2)}) copy-start(f32[64,64]{1,0:T(8,128)} %param.17) | copy-start | bytes 49156
  7.5 145.4 %copy-start.4 = (f32[1,1,32,64]{3,2,1,0:T(8,128)S(1)}, f32[1,1,32,64]{3,2,1,0:T(8,128)}, u32[]{:S(2)}) copy-start(f32[1,1,32,64]{3,2,1,0:T(8,128)} %param.15) | copy-start | bytes 24580
  7.6 164.2 %copy-start.2 = (bf16[1,1,2048]{2,1,0:T(2,128)(2,1)S(1)}, bf16[1,1,2048]{2,1,0:T(2,128)(2,1)}, u32[]{:S(2)}) copy-start(bf16[1,1,2048]{2,1,0:T(2,128)(2,1)} %param.12) | copy-start | bytes 12292
  10.5 4.4 %collective-permute-start = (f32[3,32,384]{2,1,0:T(8,128)S(1)}, f32[3,32,384]{2,1,0:T(8,128)S(1)}, u32[]{:S(2)}, u32[]{:S(2)}) collective-permute-start(f32[3,32,384]{2,1,0:T(8,128)S(1)} %get-tuple-element.13), channel_id=1, source_target_pairs={{0,1},{2,3},{4,5},{6,7},{8,9},{10,11},{12,13},{14,15},{16,17},{18,... | collective-permute-start | bytes 442376 | tf_op jit(solution)/shard_map/ppermute | solution.py:10
  11.8 4.0 %collective-permute-start.1 = (f32[3,32,384]{2,1,0:T(8,128)S(1)}, f32[3,32,384]{2,1,0:T(8,128)S(1)}, u32[]{:S(2)}, u32[]{:S(2)}) collective-permute-start(f32[3,32,384]{2,1,0:T(8,128)S(1)} %get-tuple-element.14), channel_id=1, source_target_pairs={{1,0},{3,2},{5,4},{7,6},{9,8},{11,10},{13,12},{15,14},{17,16},{19,... | collective-permute-start | bytes 442376 | tf_op jit(solution)/shard_map/ppermute | solution.py:10
  15.8 5.3 %collective-permute-start.2 = (f32[32,384]{1,0:T(8,128)S(1)}, f32[32,384]{1,0:T(8,128)S(1)}, u32[]{:S(2)}, u32[]{:S(2)}) collective-permute-start(f32[32,384]{1,0:T(8,128)S(1)} %get-tuple-element.15), channel_id=1, source_target_pairs={{0,2},{2,4},{4,6},{6,8},{8,10},{10,12},{12,14},{14,16},{16,18},{18... | collective-permute-start | bytes 147464 | tf_op jit(solution)/shard_map/ppermute | solution.py:10
  19.0 6.6 %collective-permute-start.3 = (f32[32,384]{1,0:T(8,128)S(1)}, f32[32,384]{1,0:T(8,128)S(1)}, u32[]{:S(2)}, u32[]{:S(2)}) collective-permute-start(f32[32,384]{1,0:T(8,128)S(1)} %get-tuple-element.16), channel_id=1, source_target_pairs={{2,0},{4,2},{6,4},{8,6},{10,8},{12,10},{14,12},{16,14},{18,16},{20... | collective-permute-start | bytes 147464 | tf_op jit(solution)/shard_map/ppermute | solution.py:10
  30.1 144.4 %copy-start.6 = (bf16[1,1,2048,384]{3,2,1,0:T(8,128)(2,1)S(1)}, bf16[1,1,2048,384]{3,2,1,0:T(8,128)(2,1)}, u32[]{:S(2)}) copy-start(bf16[1,1,2048,384]{3,2,1,0:T(8,128)(2,1)} %param.9) | copy-start | bytes 4718596
  153.2 6.6 %collective-permute-start.4 = (f32[1,1,32,384]{3,2,1,0:T(8,128)S(1)}, f32[1,1,32,384]{3,2,1,0:T(8,128)S(1)}, u32[]{:S(2)}, u32[]{:S(2)}) collective-permute-start(f32[1,1,32,384]{3,2,1,0:T(8,128)S(1)} %fusion.11), channel_id=1, source_target_pairs={{0,2},{2,4},{4,6},{6,8},{8,10},{10,12},{12,14},{14,16},{16,18},{18... | collective-permute-start | bytes 147464 | tf_op jit(solution)/shard_map/ppermute | solution.py:18
  157.8 6.6 %collective-permute-start.5 = (f32[1,1,32,384]{3,2,1,0:T(8,128)S(1)}, f32[1,1,32,384]{3,2,1,0:T(8,128)S(1)}, u32[]{:S(2)}, u32[]{:S(2)}) collective-permute-start(f32[1,1,32,384]{3,2,1,0:T(8,128)S(1)} %fusion.11), channel_id=1, source_target_pairs={{2,0},{4,2},{6,4},{8,6},{10,8},{12,10},{14,12},{16,14},{18,16},{20... | collective-permute-start | bytes 147464 | tf_op jit(solution)/shard_map/ppermute | solution.py:21
  164.5 7.3 %collective-permute-start.6 = (f32[3,1,32,384]{3,2,1,0:T(8,128)S(1)}, f32[3,1,32,384]{3,2,1,0:T(8,128)S(1)}, u32[]{:S(2)}, u32[]{:S(2)}) collective-permute-start(f32[3,1,32,384]{3,2,1,0:T(8,128)S(1)} %pad_maximum_fusion.1), channel_id=1, source_target_pairs={{0,1},{2,3},{4,5},{6,7},{8,9},{10,11},{12,13},{14,15},{16,17},{18,... | collective-permute-start | bytes 442376 | tf_op jit(solution)/shard_map/ppermute | solution.py:18
  165.8 6.9 %collective-permute-start.7 = (f32[3,1,32,384]{3,2,1,0:T(8,128)S(1)}, f32[3,1,32,384]{3,2,1,0:T(8,128)S(1)}, u32[]{:S(2)}, u32[]{:S(2)}) collective-permute-start(f32[3,1,32,384]{3,2,1,0:T(8,128)S(1)} %pad_maximum_fusion.1), channel_id=1, source_target_pairs={{1,0},{3,2},{5,4},{7,6},{9,8},{11,10},{13,12},{15,14},{17,16},{19,... | collective-permute-start | bytes 442376 | tf_op jit(solution)/shard_map/ppermute | solution.py:21
  182.2 38.0 %collective-permute-start.10 = (bf16[512,384]{0,1:T(8,128)(2,1)S(1)}, bf16[512,384]{0,1:T(8,128)(2,1)S(1)}, u32[]{:S(2)}, u32[]{:S(2)}) collective-permute-start(bf16[512,384]{0,1:T(8,128)(2,1)S(1)} %get-tuple-element.11), channel_id=1, source_target_pairs={{0,1},{2,3},{4,5},{6,7},{8,9},{10,11},{12,13},{14,15},{16,17},{18,... | collective-permute-start | bytes 1179656 | tf_op jit(solution)/shard_map/ppermute | solution.py:10
  183.5 36.7 %collective-permute-start.11 = (bf16[512,384]{0,1:T(8,128)(2,1)S(1)}, bf16[512,384]{0,1:T(8,128)(2,1)S(1)}, u32[]{:S(2)}, u32[]{:S(2)}) collective-permute-start(bf16[512,384]{0,1:T(8,128)(2,1)S(1)} %get-tuple-element.10), channel_id=1, source_target_pairs={{1,0},{3,2},{5,4},{7,6},{9,8},{11,10},{13,12},{15,14},{17,16},{19,... | collective-permute-start | bytes 1179656 | tf_op jit(solution)/shard_map/ppermute | solution.py:10
  186.6 33.6 %collective-permute-start.8 = (bf16[512,384]{0,1:T(8,128)(2,1)S(1)}, bf16[512,384]{0,1:T(8,128)(2,1)S(1)}, u32[]{:S(2)}, u32[]{:S(2)}) collective-permute-start(bf16[512,384]{0,1:T(8,128)(2,1)S(1)} %get-tuple-element.9), channel_id=1, source_target_pairs={{0,2},{2,4},{4,6},{6,8},{8,10},{10,12},{12,14},{14,16},{16,18},{18... | collective-permute-start | bytes 1179656 | tf_op jit(solution)/shard_map/ppermute | solution.py:10
  188.5 31.7 %collective-permute-start.9 = (bf16[512,384]{0,1:T(8,128)(2,1)S(1)}, bf16[512,384]{0,1:T(8,128)(2,1)S(1)}, u32[]{:S(2)}, u32[]{:S(2)}) collective-permute-start(bf16[512,384]{0,1:T(8,128)(2,1)S(1)} %get-tuple-element.12), channel_id=1, source_target_pairs={{2,0},{4,2},{6,4},{8,6},{10,8},{12,10},{14,12},{16,14},{18,16},{20... | collective-permute-start | bytes 1179656 | tf_op jit(solution)/shard_map/ppermute | solution.py:10
  191.9 15.8 %collective-permute-start.12 = (bf16[512]{0:T(512)(128)(2,1)S(1)}, bf16[512]{0:T(512)(128)(2,1)S(1)}, u32[]{:S(2)}, u32[]{:S(2)}) collective-permute-start(bf16[512]{0:T(512)(128)(2,1)S(1)} %get-tuple-element.5), channel_id=1, source_target_pairs={{0,2},{2,4},{4,6},{6,8},{8,10},{10,12},{12,14},{14,16},{16,18},{18... | collective-permute-start | bytes 3080 | tf_op jit(solution)/shard_map/ppermute | solution.py:10
  207.7 6.1 %collective-permute-start.13 = (bf16[512]{0:T(512)(128)(2,1)S(1)}, bf16[512]{0:T(512)(128)(2,1)S(1)}, u32[]{:S(2)}, u32[]{:S(2)}) collective-permute-start(bf16[512]{0:T(512)(128)(2,1)S(1)} %get-tuple-element.6), channel_id=1, source_target_pairs={{2,0},{4,2},{6,4},{8,6},{10,8},{12,10},{14,12},{16,14},{18,16},{20... | collective-permute-start | bytes 3080 | tf_op jit(solution)/shard_map/ppermute | solution.py:10
  213.8 3.5 %collective-permute-start.14 = (bf16[512]{0:T(512)(128)(2,1)S(1)}, bf16[512]{0:T(512)(128)(2,1)S(1)}, u32[]{:S(2)}, u32[]{:S(2)}) collective-permute-start(bf16[512]{0:T(512)(128)(2,1)S(1)} %get-tuple-element.8), channel_id=1, source_target_pairs={{0,1},{2,3},{4,5},{6,7},{8,9},{10,11},{12,13},{14,15},{16,17},{18,... | collective-permute-start | bytes 3080 | tf_op jit(solution)/shard_map/ppermute | solution.py:10
  217.3 2.9 %collective-permute-start.15 = (bf16[512]{0:T(512)(128)(2,1)S(1)}, bf16[512]{0:T(512)(128)(2,1)S(1)}, u32[]{:S(2)}, u32[]{:S(2)}) collective-permute-start(bf16[512]{0:T(512)(128)(2,1)S(1)} %get-tuple-element.7), channel_id=1, source_target_pairs={{1,0},{3,2},{5,4},{7,6},{9,8},{11,10},{13,12},{15,14},{17,16},{19,... | collective-permute-start | bytes 3080 | tf_op jit(solution)/shard_map/ppermute | solution.py:10
Sparse Core Ops, SparseCore 0:
  26.9 124.3 all-reduce.1
where the time goes:
time: 230 us; the launch traced here: 229 us
  waiting for transfers between devices  152 us (66%)
  starting transfers between devices  42 us (18%)
  matrix products  15.1 us (7%)
  between operations  13.8 us (6%)
  blocking collectives  3.32 us (1%)
    psum x1, waiting for transfers between devices, local(): lax.psum(jnp.einsum('cl,cr->lr', level_phi, assembled, precision=highest)...  121 us
    ppermute x12, starting transfers between devices, passed_along(): return lax.ppermute(block, axis, route)  28.2 us
    ppermute x12, waiting for transfers between devices, passed_along(): return lax.ppermute(block, axis, route)  24.7 us
    ppermute x2, starting transfers between devices, extended(): lax.ppermute(lax.slice_in_dim(block, 0, width, axis=dim), axis, backward)  7.86 us
    dot_general x1, matrix products, local(): jnp.dot(local_inverse[0, 0], masked, preferred_element_type=jnp.float32)  7.52 us
    ppermute x2, starting transfers between devices, extended(): lax.ppermute(lax.slice_in_dim(block, block.shape[dim] - width, None, axis...  5.93 us
    ppermute x2, waiting for transfers between devices, extended(): lax.ppermute(lax.slice_in_dim(block, 0, width, axis=dim), axis, backward)  5.64 us
  transfers between devices with their start and end apart: 17, of which 9 were waited for; matrix products, arithmetic and copies ran while one was open for 0% of the time, Pallas kernels for 0%

commit v1 on v0

--- a/solution.py
+++ b/solution.py
@@ -68,8 +68,11 @@
     from_above_x = passed_along(along_x[0], "gx", -1)
     assembled = along_x[1] + from_below_x + from_above_x
     level_phi = level_basis[0, 0]
-    top_rhs = lax.psum(
-        jnp.einsum("cl,cr->lr", level_phi, assembled, precision=highest), ("gx", "gy")
+    top_rhs = jnp.sum(
+        lax.all_gather(
+            jnp.einsum("cl,cr->lr", level_phi, assembled, precision=highest), ("gx", "gy")
+        ),
+        axis=0,
     )
     top_value = jnp.dot(top_inverse, top_rhs, precision=highest)
     block_rhs = lax.all_gather(assembled, "gy", axis=0, tiled=True)

time: 230 us -> 162 us (0.70)
  waiting for transfers between devices: 152 us -> 86.5 us
  starting transfers between devices: 42 us -> 38.4 us
    psum x1 -> x0, waiting for transfers between devices: 121 us -> none  [local(): lax.psum(jnp.einsum('cl,cr->lr', level_phi, assembled, precision=highest)...]
    all_gather x0 -> x1, waiting for transfers between devices: none -> 56.7 us  [local(): lax.all_gather(jnp.einsum('cl,cr->lr', level_phi, assembled, precision=hi...]
where the time goes in v1:
time: 162 us
  waiting for transfers between devices  86.5 us (53%)
  starting transfers between devices  38.4 us (24%)
  matrix products  14.1 us (9%)
  between operations  13.8 us (9%)
  other arithmetic  3.59 us (2%)
  blocking collectives  3.32 us (2%)
  local copies, waits for them, and re-layouts  1.97 us (1%)
    all_gather x1, waiting for transfers between devices, local(): lax.all_gather(jnp.einsum('cl,cr->lr', level_phi, assembled, precision=hi...  56.7 us
    ppermute x12, starting transfers between devices, passed_along(): return lax.ppermute(block, axis, route)  28.2 us
    ppermute x12, waiting for transfers between devices, passed_along(): return lax.ppermute(block, axis, route)  24.7 us
    dot_general x1, matrix products, local(): jnp.dot(local_inverse[0, 0], masked, preferred_element_type=jnp.float32)  7.52 us
    ppermute x2, starting transfers between devices, extended(): lax.ppermute(lax.slice_in_dim(block, 0, width, axis=dim), axis, backward)  6.03 us
    ppermute x2, waiting for transfers between devices, extended(): lax.ppermute(lax.slice_in_dim(block, 0, width, axis=dim), axis, backward)  5.14 us
    ppermute x2, starting transfers between devices, extended(): lax.ppermute(lax.slice_in_dim(block, block.shape[dim] - width, None, axis...  4.16 us
    all_gather x1, blocking collectives, local(): block_rhs = lax.all_gather(assembled, 'gy', axis=0, tiled=True)  3.32 us
  transfers between devices with their start and end apart: 17, of which 9 were waited for; matrix products, arithmetic and copies ran while one was open for 0% of the time, Pallas kernels for 0%

profile of v1, /device:TPU:7, one launch (start us, length us, event | category | flops | bytes accessed | tf_op | source)
XLA Modules:
  0.0 161.7 jit_solution(5696783777811926736)
XLA Ops:
  7.5 2.4 %fusion.7 = f32[384,96]{1,0:T(8,128)S(1)} fusion(bf16[1,1,2048,384]{3,2,1,0:T(8,128)(2,1)} %param.9, pred[2048]{0:T(1024)(128)(4,1)S(1)} %fusion.29, bf16[1,1,96,2048]{3,2,1,0:T(8,128)(2,1)S(1)} %copy-done), kind=kOutput, calls=%fused_computation.5 | convolution fusion | flops 151781376 | bytes 2115584 | tf_op jit(solution)/shard_map/dot_general | solution.py:57
  10.5 1.3 collective-permute-start
  11.8 3.0 %collective-permute-start.1 = (f32[3,32,384]{2,1,0:T(8,128)S(1)}, f32[3,32,384]{2,1,0:T(8,128)S(1)}, u32[]{:S(2)}, u32[]{:S(2)}) collective-permute-start(f32[3,32,384]{2,1,0:T(8,128)S(1)} %get-tuple-element.14), channel_id=1, source_target_pairs={{1,0},{3,2},{5,4},{7,6},{9,8},{11,10},{13,12},{15,14},{17,16},{19,... | collective-permute-start | bytes 442376 | tf_op jit(solution)/shard_map/ppermute | solution.py:10
  14.8 1.0 collective-permute-done.1
  15.8 3.1 %collective-permute-start.2 = (f32[32,384]{1,0:T(8,128)S(1)}, f32[32,384]{1,0:T(8,128)S(1)}, u32[]{:S(2)}, u32[]{:S(2)}) collective-permute-start(f32[32,384]{1,0:T(8,128)S(1)} %get-tuple-element.15), channel_id=1, source_target_pairs={{0,2},{2,4},{4,6},{6,8},{8,10},{10,12},{12,14},{14,16},{16,18},{18... | collective-permute-start | bytes 147464 | tf_op jit(solution)/shard_map/ppermute | solution.py:10
  19.0 2.2 %collective-permute-start.3 = (f32[32,384]{1,0:T(8,128)S(1)}, f32[32,384]{1,0:T(8,128)S(1)}, u32[]{:S(2)}, u32[]{:S(2)}) collective-permute-start(f32[32,384]{1,0:T(8,128)S(1)} %get-tuple-element.16), channel_id=1, source_target_pairs={{2,0},{4,2},{6,4},{8,6},{10,8},{12,10},{14,12},{16,14},{18,16},{20... | collective-permute-start | bytes 147464 | tf_op jit(solution)/shard_map/ppermute | solution.py:10
  21.2 4.5 %collective-permute-done.3 = f32[32,384]{1,0:T(8,128)S(1)} collective-permute-done((f32[32,384]{1,0:T(8,128)S(1)}, f32[32,384]{1,0:T(8,128)S(1)}, u32[]{:S(2)}, u32[]{:S(2)}) %collective-permute-start.3) | collective-permute-done | bytes 49184 | tf_op jit(solution)/shard_map/ppermute | solution.py:10
  25.6 0.9 convolution_bitcast_fusion
  26.6 3.3 %all_gather.9 = f32[64,384]{1,0:T(8,128)S(1)} all-gather(f32[32,384]{1,0:T(8,128)S(1)} %fusion.24), channel_id=1, replica_groups=mesh['gx'=16,'gy'=2] {'gy'}, dimensions={0}, use_global_device_ids=true | all-gather | bytes 147456 | tf_op jit(solution)/shard_map/all_gather | solution.py:78
  29.9 56.7 %all-gather.3.cloned.1.call-done = f32[2048,384]{1,0:T(8,128)} async-done(((f32[64,384]{1,0:T(8,128)}), f32[2048,384]{1,0:T(8,128)}) %all-gather.3.cloned.1.call-update) | async-done | bytes 3145744 | tf_op jit(solution)/shard_map/all_gather | solution.py:72
  86.6 2.0 %reduce_sum.19 = f32[64,384]{1,0:T(8,128)S(1)} reduce(f32[32,64,384]{2,1,0:T(8,128)} %bitcast.73, f32[]{:T(128)} %constant.35.clone.1), dimensions={0}, to_apply=%region_1.2 | reduce | flops 761856 | bytes 3244036 | tf_op jit(solution)/shard_map/reduce_sum | solution.py:71
  89.7 2.9 %collective-permute-start.4 = (f32[1,1,32,384]{3,2,1,0:T(8,128)S(1)}, f32[1,1,32,384]{3,2,1,0:T(8,128)S(1)}, u32[]{:S(2)}, u32[]{:S(2)}) collective-permute-start(f32[1,1,32,384]{3,2,1,0:T(8,128)S(1)} %fusion.11), channel_id=1, source_target_pairs={{0,2},{2,4},{4,6},{6,8},{8,10},{10,12},{12,14},{14,16},{16,18},{18... | collective-permute-start | bytes 147464 | tf_op jit(solution)/shard_map/ppermute | solution.py:18
  92.6 2.4 %collective-permute-start.5 = (f32[1,1,32,384]{3,2,1,0:T(8,128)S(1)}, f32[1,1,32,384]{3,2,1,0:T(8,128)S(1)}, u32[]{:S(2)}, u32[]{:S(2)}) collective-permute-start(f32[1,1,32,384]{3,2,1,0:T(8,128)S(1)} %fusion.11), channel_id=1, source_target_pairs={{2,0},{4,2},{6,4},{8,6},{10,8},{12,10},{14,12},{16,14},{18,16},{20... | collective-permute-start | bytes 147464 | tf_op jit(solution)/shard_map/ppermute | solution.py:21
  95.0 4.2 %collective-permute-done.5 = f32[1,1,32,384]{3,2,1,0:T(8,128)S(1)} collective-permute-done((f32[1,1,32,384]{3,2,1,0:T(8,128)S(1)}, f32[1,1,32,384]{3,2,1,0:T(8,128)S(1)}, u32[]{:S(2)}, u32[]{:S(2)}) %collective-permute-start.5) | collective-permute-done | bytes 49184 | tf_op jit(solution)/shard_map/ppermute | solution.py:21
  99.3 1.3 collective-permute-start.6
  100.6 3.6 %collective-permute-start.7 = (f32[3,1,32,384]{3,2,1,0:T(8,128)S(1)}, f32[3,1,32,384]{3,2,1,0:T(8,128)S(1)}, u32[]{:S(2)}, u32[]{:S(2)}) collective-permute-start(f32[3,1,32,384]{3,2,1,0:T(8,128)S(1)} %pad_maximum_fusion.1), channel_id=1, source_target_pairs={{1,0},{3,2},{5,4},{7,6},{9,8},{11,10},{13,12},{15,14},{17,16},{19,... | collective-permute-start | bytes 442376 | tf_op jit(solution)/shard_map/ppermute | solution.py:21
  104.2 0.9 collective-permute-done.7
  105.6 1.4 fusion.12
  107.0 7.5 %fusion.4 = bf16[2048,384]{0,1:T(8,128)(2,1)S(1)} fusion(f32[384,2048]{1,0:T(8,128)S(1)} %fusion.12, bf16[1,1,2048,2048]{3,2,1,0:T(8,128)(2,1)} %param.10, f32[2048]{0:T(1024)S(1)} %bitcast.77, pred[2048]{0:T(1024)(128)(4,1)S(1)} %fusion.29, bf16[1,1,2048,384]{3,2,1,0:T(8,128)(2,1)S(1)} %copy-done.6), kind=kOutput, calls=%fused_computation.4 | convolution fusion | flops 3226730496 | bytes 14690304 | tf_op jit(solution)/shard_map/dot_general | solution.py:55
  114.7 1.3 collective-permute-start.10
  116.0 3.1 %collective-permute-start.11 = (bf16[512,384]{0,1:T(8,128)(2,1)S(1)}, bf16[512,384]{0,1:T(8,128)(2,1)S(1)}, u32[]{:S(2)}, u32[]{:S(2)}) collective-permute-start(bf16[512,384]{0,1:T(8,128)(2,1)S(1)} %get-tuple-element.10), channel_id=1, source_target_pairs={{1,0},{3,2},{5,4},{7,6},{9,8},{11,10},{13,12},{15,14},{17,16},{19,... | collective-permute-start | bytes 1179656 | tf_op jit(solution)/shard_map/ppermute | solution.py:10
  119.1 1.9 %collective-permute-start.8 = (bf16[512,384]{0,1:T(8,128)(2,1)S(1)}, bf16[512,384]{0,1:T(8,128)(2,1)S(1)}, u32[]{:S(2)}, u32[]{:S(2)}) collective-permute-start(bf16[512,384]{0,1:T(8,128)(2,1)S(1)} %get-tuple-element.9), channel_id=1, source_target_pairs={{0,2},{2,4},{4,6},{6,8},{8,10},{10,12},{12,14},{14,16},{16,18},{18... | collective-permute-start | bytes 1179656 | tf_op jit(solution)/shard_map/ppermute | solution.py:10
  121.0 3.4 %collective-permute-start.9 = (bf16[512,384]{0,1:T(8,128)(2,1)S(1)}, bf16[512,384]{0,1:T(8,128)(2,1)S(1)}, u32[]{:S(2)}, u32[]{:S(2)}) collective-permute-start(bf16[512,384]{0,1:T(8,128)(2,1)S(1)} %get-tuple-element.12), channel_id=1, source_target_pairs={{2,0},{4,2},{6,4},{8,6},{10,8},{12,10},{14,12},{16,14},{18,16},{20... | collective-permute-start | bytes 1179656 | tf_op jit(solution)/shard_map/ppermute | solution.py:10
  124.4 3.7 %collective-permute-start.12 = (bf16[512]{0:T(512)(128)(2,1)S(1)}, bf16[512]{0:T(512)(128)(2,1)S(1)}, u32[]{:S(2)}, u32[]{:S(2)}) collective-permute-start(bf16[512]{0:T(512)(128)(2,1)S(1)} %get-tuple-element.5), channel_id=1, source_target_pairs={{0,2},{2,4},{4,6},{6,8},{8,10},{10,12},{12,14},{14,16},{16,18},{18... | collective-permute-start | bytes 3080 | tf_op jit(solution)/shard_map/ppermute | solution.py:10
  128.1 12.1 %collective-permute-done.12 = bf16[512]{0:T(512)(128)(2,1)S(1)} collective-permute-done((bf16[512]{0:T(512)(128)(2,1)S(1)}, bf16[512]{0:T(512)(128)(2,1)S(1)}, u32[]{:S(2)}, u32[]{:S(2)}) %collective-permute-start.12) | collective-permute-done | bytes 1056 | tf_op jit(solution)/shard_map/ppermute | solution.py:10
  140.2 1.9 %collective-permute-start.13 = (bf16[512]{0:T(512)(128)(2,1)S(1)}, bf16[512]{0:T(512)(128)(2,1)S(1)}, u32[]{:S(2)}, u32[]{:S(2)}) collective-permute-start(bf16[512]{0:T(512)(128)(2,1)S(1)} %get-tuple-element.6), channel_id=1, source_target_pairs={{2,0},{4,2},{6,4},{8,6},{10,8},{12,10},{14,12},{16,14},{18,16},{20... | collective-permute-start | bytes 3080 | tf_op jit(solution)/shard_map/ppermute | solution.py:10
  142.1 4.2 %collective-permute-done.13 = bf16[512]{0:T(512)(128)(2,1)S(1)} collective-permute-done((bf16[512]{0:T(512)(128)(2,1)S(1)}, bf16[512]{0:T(512)(128)(2,1)S(1)}, u32[]{:S(2)}, u32[]{:S(2)}) %collective-permute-start.13) | collective-permute-done | bytes 1056 | tf_op jit(solution)/shard_map/ppermute | solution.py:10
  146.3 1.3 collective-permute-start.14
  147.6 2.2 %collective-permute-done.14 = bf16[512]{0:T(512)(128)(2,1)S(1)} collective-permute-done((bf16[512]{0:T(512)(128)(2,1)S(1)}, bf16[512]{0:T(512)(128)(2,1)S(1)}, u32[]{:S(2)}, u32[]{:S(2)}) %collective-permute-start.14) | collective-permute-done | bytes 1056 | tf_op jit(solution)/shard_map/ppermute | solution.py:10
  149.8 2.1 %collective-permute-start.15 = (bf16[512]{0:T(512)(128)(2,1)S(1)}, bf16[512]{0:T(512)(128)(2,1)S(1)}, u32[]{:S(2)}, u32[]{:S(2)}) collective-permute-start(bf16[512]{0:T(512)(128)(2,1)S(1)} %get-tuple-element.7), channel_id=1, source_target_pairs={{1,0},{3,2},{5,4},{7,6},{9,8},{11,10},{13,12},{15,14},{17,16},{19,... | collective-permute-start | bytes 3080 | tf_op jit(solution)/shard_map/ppermute | solution.py:10
  151.8 0.8 collective-permute-done.15
  153.3 1.6 copy.15
  (43 shorter events, 3.8 us)
Async XLA Ops:
  6.5 1.0 copy-start
  6.5 3.4 %copy-start.5 = (s32[1,1,96]{2,1,0:T(1,128)S(1)}, s32[1,1,96]{2,1,0:T(1,128)}, u32[]{:S(2)}) copy-start(s32[1,1,96]{2,1,0:T(1,128)} %param.14) | copy-start | bytes 1156
  6.5 19.1 %copy-start.1 = (f32[1,1,32,64]{3,2,1,0:T(8,128)S(1)}, f32[1,1,32,64]{3,2,1,0:T(8,128)}, u32[]{:S(2)}) copy-start(f32[1,1,32,64]{3,2,1,0:T(8,128)} %param.16) | copy-start | bytes 24580
  6.5 80.1 %all-gather.3.cloned.1.call-start = ((), (), s32[]{:S(2)}) async-start(), calls=%async_computation | async-start | bytes 3244032 | tf_op jit(solution)/shard_map/all_gather | solution.py:72
  9.9 78.7 %copy-start.2 = (f32[64,64]{1,0:T(8,128)S(1)}, f32[64,64]{1,0:T(8,128)}, u32[]{:S(2)}) copy-start(f32[64,64]{1,0:T(8,128)} %param.17) | copy-start | bytes 49156
  10.0 79.6 %copy-start.4 = (f32[1,1,32,64]{3,2,1,0:T(8,128)S(1)}, f32[1,1,32,64]{3,2,1,0:T(8,128)}, u32[]{:S(2)}) copy-start(f32[1,1,32,64]{3,2,1,0:T(8,128)} %param.15) | copy-start | bytes 24580
  10.4 93.8 %copy-start.3 = (bf16[1,1,2048]{2,1,0:T(2,128)(2,1)S(1)}, bf16[1,1,2048]{2,1,0:T(2,128)(2,1)}, u32[]{:S(2)}) copy-start(bf16[1,1,2048]{2,1,0:T(2,128)(2,1)} %param.12) | copy-start | bytes 12292
  10.5 4.4 %collective-permute-start = (f32[3,32,384]{2,1,0:T(8,128)S(1)}, f32[3,32,384]{2,1,0:T(8,128)S(1)}, u32[]{:S(2)}, u32[]{:S(2)}) collective-permute-start(f32[3,32,384]{2,1,0:T(8,128)S(1)} %get-tuple-element.13), channel_id=1, source_target_pairs={{0,1},{2,3},{4,5},{6,7},{8,9},{10,11},{12,13},{14,15},{16,17},{18,... | collective-permute-start | bytes 442376 | tf_op jit(solution)/shard_map/ppermute | solution.py:10
  11.8 4.0 %collective-permute-start.1 = (f32[3,32,384]{2,1,0:T(8,128)S(1)}, f32[3,32,384]{2,1,0:T(8,128)S(1)}, u32[]{:S(2)}, u32[]{:S(2)}) collective-permute-start(f32[3,32,384]{2,1,0:T(8,128)S(1)} %get-tuple-element.14), channel_id=1, source_target_pairs={{1,0},{3,2},{5,4},{7,6},{9,8},{11,10},{13,12},{15,14},{17,16},{19,... | collective-permute-start | bytes 442376 | tf_op jit(solution)/shard_map/ppermute | solution.py:10
  15.8 5.3 %collective-permute-start.2 = (f32[32,384]{1,0:T(8,128)S(1)}, f32[32,384]{1,0:T(8,128)S(1)}, u32[]{:S(2)}, u32[]{:S(2)}) collective-permute-start(f32[32,384]{1,0:T(8,128)S(1)} %get-tuple-element.15), channel_id=1, source_target_pairs={{0,2},{2,4},{4,6},{6,8},{8,10},{10,12},{12,14},{14,16},{16,18},{18... | collective-permute-start | bytes 147464 | tf_op jit(solution)/shard_map/ppermute | solution.py:10
  19.0 6.6 %collective-permute-start.3 = (f32[32,384]{1,0:T(8,128)S(1)}, f32[32,384]{1,0:T(8,128)S(1)}, u32[]{:S(2)}, u32[]{:S(2)}) collective-permute-start(f32[32,384]{1,0:T(8,128)S(1)} %get-tuple-element.16), channel_id=1, source_target_pairs={{2,0},{4,2},{6,4},{8,6},{10,8},{12,10},{14,12},{16,14},{18,16},{20... | collective-permute-start | bytes 147464 | tf_op jit(solution)/shard_map/ppermute | solution.py:10
  88.7 18.4 %copy-start.6 = (bf16[1,1,2048,384]{3,2,1,0:T(8,128)(2,1)S(1)}, bf16[1,1,2048,384]{3,2,1,0:T(8,128)(2,1)}, u32[]{:S(2)}) copy-start(bf16[1,1,2048,384]{3,2,1,0:T(8,128)(2,1)} %param.9) | copy-start | bytes 4718596
  89.7 5.3 %collective-permute-start.4 = (f32[1,1,32,384]{3,2,1,0:T(8,128)S(1)}, f32[1,1,32,384]{3,2,1,0:T(8,128)S(1)}, u32[]{:S(2)}, u32[]{:S(2)}) collective-permute-start(f32[1,1,32,384]{3,2,1,0:T(8,128)S(1)} %fusion.11), channel_id=1, source_target_pairs={{0,2},{2,4},{4,6},{6,8},{8,10},{10,12},{12,14},{14,16},{16,18},{18... | collective-permute-start | bytes 147464 | tf_op jit(solution)/shard_map/ppermute | solution.py:18
  92.6 6.6 %collective-permute-start.5 = (f32[1,1,32,384]{3,2,1,0:T(8,128)S(1)}, f32[1,1,32,384]{3,2,1,0:T(8,128)S(1)}, u32[]{:S(2)}, u32[]{:S(2)}) collective-permute-start(f32[1,1,32,384]{3,2,1,0:T(8,128)S(1)} %fusion.11), channel_id=1, source_target_pairs={{2,0},{4,2},{6,4},{8,6},{10,8},{12,10},{14,12},{16,14},{18,16},{20... | collective-permute-start | bytes 147464 | tf_op jit(solution)/shard_map/ppermute | solution.py:21
  99.3 5.0 %collective-permute-start.6 = (f32[3,1,32,384]{3,2,1,0:T(8,128)S(1)}, f32[3,1,32,384]{3,2,1,0:T(8,128)S(1)}, u32[]{:S(2)}, u32[]{:S(2)}) collective-permute-start(f32[3,1,32,384]{3,2,1,0:T(8,128)S(1)} %pad_maximum_fusion.1), channel_id=1, source_target_pairs={{0,1},{2,3},{4,5},{6,7},{8,9},{10,11},{12,13},{14,15},{16,17},{18,... | collective-permute-start | bytes 442376 | tf_op jit(solution)/shard_map/ppermute | solution.py:18
  100.6 4.6 %collective-permute-start.7 = (f32[3,1,32,384]{3,2,1,0:T(8,128)S(1)}, f32[3,1,32,384]{3,2,1,0:T(8,128)S(1)}, u32[]{:S(2)}, u32[]{:S(2)}) collective-permute-start(f32[3,1,32,384]{3,2,1,0:T(8,128)S(1)} %pad_maximum_fusion.1), channel_id=1, source_target_pairs={{1,0},{3,2},{5,4},{7,6},{9,8},{11,10},{13,12},{15,14},{17,16},{19,... | collective-permute-start | bytes 442376 | tf_op jit(solution)/shard_map/ppermute | solution.py:21
  114.7 38.0 %collective-permute-start.10 = (bf16[512,384]{0,1:T(8,128)(2,1)S(1)}, bf16[512,384]{0,1:T(8,128)(2,1)S(1)}, u32[]{:S(2)}, u32[]{:S(2)}) collective-permute-start(bf16[512,384]{0,1:T(8,128)(2,1)S(1)} %get-tuple-element.11), channel_id=1, source_target_pairs={{0,1},{2,3},{4,5},{6,7},{8,9},{10,11},{12,13},{14,15},{16,17},{18,... | collective-permute-start | bytes 1179656 | tf_op jit(solution)/shard_map/ppermute | solution.py:10
  116.0 36.7 %collective-permute-start.11 = (bf16[512,384]{0,1:T(8,128)(2,1)S(1)}, bf16[512,384]{0,1:T(8,128)(2,1)S(1)}, u32[]{:S(2)}, u32[]{:S(2)}) collective-permute-start(bf16[512,384]{0,1:T(8,128)(2,1)S(1)} %get-tuple-element.10), channel_id=1, source_target_pairs={{1,0},{3,2},{5,4},{7,6},{9,8},{11,10},{13,12},{15,14},{17,16},{19,... | collective-permute-start | bytes 1179656 | tf_op jit(solution)/shard_map/ppermute | solution.py:10
  119.1 33.6 %collective-permute-start.8 = (bf16[512,384]{0,1:T(8,128)(2,1)S(1)}, bf16[512,384]{0,1:T(8,128)(2,1)S(1)}, u32[]{:S(2)}, u32[]{:S(2)}) collective-permute-start(bf16[512,384]{0,1:T(8,128)(2,1)S(1)} %get-tuple-element.9), channel_id=1, source_target_pairs={{0,2},{2,4},{4,6},{6,8},{8,10},{10,12},{12,14},{14,16},{16,18},{18... | collective-permute-start | bytes 1179656 | tf_op jit(solution)/shard_map/ppermute | solution.py:10
  121.0 31.7 %collective-permute-start.9 = (bf16[512,384]{0,1:T(8,128)(2,1)S(1)}, bf16[512,384]{0,1:T(8,128)(2,1)S(1)}, u32[]{:S(2)}, u32[]{:S(2)}) collective-permute-start(bf16[512,384]{0,1:T(8,128)(2,1)S(1)} %get-tuple-element.12), channel_id=1, source_target_pairs={{2,0},{4,2},{6,4},{8,6},{10,8},{12,10},{14,12},{16,14},{18,16},{20... | collective-permute-start | bytes 1179656 | tf_op jit(solution)/shard_map/ppermute | solution.py:10
  124.4 15.8 %collective-permute-start.12 = (bf16[512]{0:T(512)(128)(2,1)S(1)}, bf16[512]{0:T(512)(128)(2,1)S(1)}, u32[]{:S(2)}, u32[]{:S(2)}) collective-permute-start(bf16[512]{0:T(512)(128)(2,1)S(1)} %get-tuple-element.5), channel_id=1, source_target_pairs={{0,2},{2,4},{4,6},{6,8},{8,10},{10,12},{12,14},{14,16},{16,18},{18... | collective-permute-start | bytes 3080 | tf_op jit(solution)/shard_map/ppermute | solution.py:10
  140.2 6.1 %collective-permute-start.13 = (bf16[512]{0:T(512)(128)(2,1)S(1)}, bf16[512]{0:T(512)(128)(2,1)S(1)}, u32[]{:S(2)}, u32[]{:S(2)}) collective-permute-start(bf16[512]{0:T(512)(128)(2,1)S(1)} %get-tuple-element.6), channel_id=1, source_target_pairs={{2,0},{4,2},{6,4},{8,6},{10,8},{12,10},{14,12},{16,14},{18,16},{20... | collective-permute-start | bytes 3080 | tf_op jit(solution)/shard_map/ppermute | solution.py:10
  146.3 3.5 %collective-permute-start.14 = (bf16[512]{0:T(512)(128)(2,1)S(1)}, bf16[512]{0:T(512)(128)(2,1)S(1)}, u32[]{:S(2)}, u32[]{:S(2)}) collective-permute-start(bf16[512]{0:T(512)(128)(2,1)S(1)} %get-tuple-element.8), channel_id=1, source_target_pairs={{0,1},{2,3},{4,5},{6,7},{8,9},{10,11},{12,13},{14,15},{16,17},{18,... | collective-permute-start | bytes 3080 | tf_op jit(solution)/shard_map/ppermute | solution.py:10
  149.8 2.9 %collective-permute-start.15 = (bf16[512]{0:T(512)(128)(2,1)S(1)}, bf16[512]{0:T(512)(128)(2,1)S(1)}, u32[]{:S(2)}, u32[]{:S(2)}) collective-permute-start(bf16[512]{0:T(512)(128)(2,1)S(1)} %get-tuple-element.7), channel_id=1, source_target_pairs={{1,0},{3,2},{5,4},{7,6},{9,8},{11,10},{13,12},{15,14},{17,16},{19,... | collective-permute-start | bytes 3080 | tf_op jit(solution)/shard_map/ppermute | solution.py:10
Sparse Core Ops, SparseCore 0:
  26.7 59.8 all-gather.2
